TPU v7x, 64 devices: a 2x2x8 block of a 4x4x8 slice. The times are simulated.
64 devices in a mesh: dp: 4 (over x, y), sp: 16 (over z, core).
Axes of the slice: x: 2, y: 2, z: 8, core: 2. Of those that a mesh axis runs over, the one named last changes fastest.
The devices are a block of a 4x4x8 slice.
Arguments:
- x_in: bfloat16 [32768, 4096], P(('dp', 'sp')), parts along dimension 0
- w_in: bfloat16 [4096, 16768], replicated
- a_neg: float32 [128], replicated
- dt_bias: float32 [128], replicated
- d_skip: float32 [128], replicated
- w_out: bfloat16 [8192, 4096], replicated
Outputs:
- output: bfloat16 [32768, 4096], P(('dp', 'sp')), parts along dimension 0
There are 4 independent parts. A program takes and returns all parts, laid end to end along the dimension named above; an argument that names none is the same for every part.
All inputs are finite; a program needn't handle non-finite values.
Results may differ from a plain program's by a relative error of at most 0.00322704.
Values are sent between devices in bfloat16 or wider.
A program may use at most 768 MiB of HBM per device.

v0:
```python
import jax
import jax.numpy as jnp
from jax import lax
from jax.sharding import PartitionSpec as P

SEG_LEN = 128


def combine_states(left, right):
    left_log, left_state = left
    right_log, right_state = right
    return left_log + right_log, jnp.exp(right_log)[..., None, None] * left_state + right_state


def solution(mesh):
    seq_devs = mesh.shape["sp"]
    hop_pairs = [(sender, sender + 1) for sender in range(seq_devs - 1)]
    row_spec = P(("dp", "sp"), None)

    def local_mixer(x_loc, w_in, a_neg, dt_bias, d_skip, w_out):
        inner = w_out.shape[0]
        heads = a_neg.shape[0]
        state = (w_in.shape[1] - 2 * inner - heads) // 2
        head_dim = inner // heads
        tokens = x_loc.shape[0]
        seg_count = tokens // SEG_LEN
        projected = jnp.dot(x_loc, w_in, preferred_element_type=jnp.float32).astype(jnp.bfloat16)
        z_gate = projected[:, :inner]
        x_heads = projected[:, inner:2 * inner].reshape(seg_count, SEG_LEN, heads, head_dim)
        b_mat = projected[:, 2 * inner:2 * inner + state].reshape(seg_count, SEG_LEN, state)
        c_mat = projected[:, 2 * inner + state:2 * inner + 2 * state].reshape(seg_count, SEG_LEN, state)
        dt_vals = jax.nn.softplus(projected[:, 2 * inner + 2 * state:].astype(jnp.float32) + dt_bias).reshape(seg_count, SEG_LEN, heads)
        log_cum = jnp.cumsum(dt_vals * a_neg, axis=1)
        seg_log = log_cum[:, -1, :]
        x_weighted = (x_heads * (jnp.exp(seg_log[:, None, :] - log_cum) * dt_vals)[..., None]).astype(jnp.bfloat16)
        s_seg = jnp.einsum("cshp,csn->chpn", x_weighted, b_mat, preferred_element_type=jnp.float32)
        seg_cum, h_end = lax.associative_scan(combine_states, (seg_log, s_seg), axis=0)
        s_block = h_end[-1]
        block_decay = jnp.exp(seg_cum[-1])[:, None, None]

        def pass_state(hop_index, carry):
            return lax.ppermute(block_decay * carry + s_block, "sp", hop_pairs)

        h_in = lax.fori_loop(0, seq_devs - 1, pass_state, jnp.zeros_like(s_block))
        h_start = jnp.concatenate([jnp.zeros_like(h_end[:1]), h_end[:-1]], axis=0) + jnp.exp(seg_cum - seg_log)[:, :, None, None] * h_in
        causal = jnp.arange(SEG_LEN)[:, None] >= jnp.arange(SEG_LEN)[None, :]
        mask_four = causal[None, :, :, None]
        decay_mat = jnp.where(mask_four, jnp.exp(jnp.where(mask_four, log_cum[:, :, None, :] - log_cum[:, None, :, :], 0.0)), 0.0)
        scores = jnp.einsum("ctn,csn->cts", c_mat, b_mat, preferred_element_type=jnp.float32)
        g_mat = (scores[..., None] * decay_mat * dt_vals[:, None, :, :]).astype(jnp.bfloat16)
        y_intra = jnp.einsum("ctsh,cshp->cthp", g_mat, x_heads, preferred_element_type=jnp.float32)
        y_state = jnp.einsum("ctn,chpn->cthp", c_mat, h_start.astype(jnp.bfloat16), preferred_element_type=jnp.float32) * jnp.exp(log_cum)[..., None]
        y_all = y_intra + y_state + d_skip[:, None] * x_heads
        gated = (y_all.reshape(tokens, inner) * jax.nn.silu(z_gate.astype(jnp.float32))).astype(jnp.bfloat16)
        return (x_loc.astype(jnp.float32) + jnp.dot(gated, w_out, preferred_element_type=jnp.float32)).astype(jnp.bfloat16)

    return jax.shard_map(local_mixer, mesh=mesh, in_specs=(row_spec, P(), P(), P(), P(), P()),
                         out_specs=row_spec, check_vma=False)
```

profile of v0, /device:TPU:158, one launch (start us, length us, event | category | flops | bytes accessed | tf_op | source)
XLA Modules:
  0.0 1426.2 jit_solution(7006871051915479420)
XLA Ops:
  0.0 80.4 %convolution_convert_fusion = bf16[512,16768]{1,0:T(8,128)(2,1)} fusion(bf16[512,4096]{1,0:T(8,128)(2,1)} %param.8, bf16[4096,16768]{1,0:T(8,128)(2,1)} %param.9), kind=kOutput, calls=%fused_computation.2 | convolution fusion | flops 70338674688 | bytes 158728192 | tf_op jit(solution)/shard_map/dot_general | solution.py:27
  82.2 7.6 slice.110
  89.8 23.6 %reshape.85 = bf16[4,128,128,64]{3,2,1,0:T(8,128)(2,1)} reshape(bf16[512,8192]{1,0:T(8,128)(2,1)} %slice.110) | data formatting | bytes 16777216 | tf_op jit(solution)/shard_map/reshape | solution.py:29
  113.4 22.1 %copy.23 = bf16[4,128,128,64]{1,3,2,0:T(8,128)(2,1)} copy(bf16[4,128,128,64]{3,2,1,0:T(8,128)(2,1)} %reshape.85) | data formatting | bytes 16777216 | tf_op jit(solution)/shard_map/reshape | solution.py:29
  135.5 9.8 fusion.1
  146.2 25.7 %fusion.19 = f32[4,128,64,128]{3,1,2,0:T(8,128)} fusion(bf16[4,128,128,1]{2,1,3,0:T(8,128)(2,1)S(1)} %bitcast.47, bf16[4,128,128,64]{1,3,2,0:T(8,128)(2,1)} %fusion.1), kind=kOutput, calls=%fused_computation.32 | convolution fusion | flops 1073741824 | bytes 25296896 | tf_op jit(solution)/shard_map/cshp,csn->chpn/dot_general | solution.py:36
  187.4 68.1 %pad.62 = f32[3,128,64,128]{3,1,2,0:T(8,128)} pad(f32[2,128,64,128]{3,1,2,0:T(8,128)} %pad_add_fusion, f32[]{:T(128)} %constant.8.clone.1), padding=0_0_1x0_0_0x0_0_0x0_0_0 | pad | bytes 20971524
  264.9 854.7 %while.10 = (s32[]{:T(128)}, f32[128,64,128]{2,1,0:T(8,128)}, f32[128,1,1]{0,2,1:T(1,128)S(1)}, f32[128,64,128]{2,1,0:T(8,128)}, s32[]{:T(128)}) while((s32[]{:T(128)}, f32[128,64,128]{2,1,0:T(8,128)}, f32[128,1,1]{0,2,1:T(1,128)S(1)}, f32[128,64,128]{2,1,0:T(8,128)}, s32[]{:T(128)}) %tuple.29), condition=%wide.region_2.3_spmd, body=%wide.region_1.2_spmd.sunk | while | flops 2097154 | bytes 29360740 | solution.py:44
  272.7 49.1 %collective-permute-done = f32[128,64,128]{2,1,0:T(8,128)} collective-permute-done((f32[128,64,128]{2,1,0:T(8,128)}, f32[128,64,128]{2,1,0:T(8,128)}, u32[]{:S(2)}, u32[]{:S(2)}) %collective-permute-start) | collective-permute-done | bytes 4194336 | tf_op jit(solution)/shard_map/while/body/eval_jaxpr/ppermute | solution.py:42
  329.7 49.1 %collective-permute-done = f32[128,64,128]{2,1,0:T(8,128)} collective-permute-done((f32[128,64,128]{2,1,0:T(8,128)}, f32[128,64,128]{2,1,0:T(8,128)}, u32[]{:S(2)}, u32[]{:S(2)}) %collective-permute-start) | collective-permute-done | bytes 4194336 | tf_op jit(solution)/shard_map/while/body/eval_jaxpr/ppermute | solution.py:42
  386.7 49.1 %collective-permute-done = f32[128,64,128]{2,1,0:T(8,128)} collective-permute-done((f32[128,64,128]{2,1,0:T(8,128)}, f32[128,64,128]{2,1,0:T(8,128)}, u32[]{:S(2)}, u32[]{:S(2)}) %collective-permute-start) | collective-permute-done | bytes 4194336 | tf_op jit(solution)/shard_map/while/body/eval_jaxpr/ppermute | solution.py:42
  443.7 49.1 %collective-permute-done = f32[128,64,128]{2,1,0:T(8,128)} collective-permute-done((f32[128,64,128]{2,1,0:T(8,128)}, f32[128,64,128]{2,1,0:T(8,128)}, u32[]{:S(2)}, u32[]{:S(2)}) %collective-permute-start) | collective-permute-done | bytes 4194336 | tf_op jit(solution)/shard_map/while/body/eval_jaxpr/ppermute | solution.py:42
  500.7 49.1 %collective-permute-done = f32[128,64,128]{2,1,0:T(8,128)} collective-permute-done((f32[128,64,128]{2,1,0:T(8,128)}, f32[128,64,128]{2,1,0:T(8,128)}, u32[]{:S(2)}, u32[]{:S(2)}) %collective-permute-start) | collective-permute-done | bytes 4194336 | tf_op jit(solution)/shard_map/while/body/eval_jaxpr/ppermute | solution.py:42
  557.6 49.1 %collective-permute-done = f32[128,64,128]{2,1,0:T(8,128)} collective-permute-done((f32[128,64,128]{2,1,0:T(8,128)}, f32[128,64,128]{2,1,0:T(8,128)}, u32[]{:S(2)}, u32[]{:S(2)}) %collective-permute-start) | collective-permute-done | bytes 4194336 | tf_op jit(solution)/shard_map/while/body/eval_jaxpr/ppermute | solution.py:42
  614.6 49.1 %collective-permute-done = f32[128,64,128]{2,1,0:T(8,128)} collective-permute-done((f32[128,64,128]{2,1,0:T(8,128)}, f32[128,64,128]{2,1,0:T(8,128)}, u32[]{:S(2)}, u32[]{:S(2)}) %collective-permute-start) | collective-permute-done | bytes 4194336 | tf_op jit(solution)/shard_map/while/body/eval_jaxpr/ppermute | solution.py:42
  671.6 49.1 %collective-permute-done = f32[128,64,128]{2,1,0:T(8,128)} collective-permute-done((f32[128,64,128]{2,1,0:T(8,128)}, f32[128,64,128]{2,1,0:T(8,128)}, u32[]{:S(2)}, u32[]{:S(2)}) %collective-permute-start) | collective-permute-done | bytes 4194336 | tf_op jit(solution)/shard_map/while/body/eval_jaxpr/ppermute | solution.py:42
  728.6 49.1 %collective-permute-done = f32[128,64,128]{2,1,0:T(8,128)} collective-permute-done((f32[128,64,128]{2,1,0:T(8,128)}, f32[128,64,128]{2,1,0:T(8,128)}, u32[]{:S(2)}, u32[]{:S(2)}) %collective-permute-start) | collective-permute-done | bytes 4194336 | tf_op jit(solution)/shard_map/while/body/eval_jaxpr/ppermute | solution.py:42
  785.6 49.1 %collective-permute-done = f32[128,64,128]{2,1,0:T(8,128)} collective-permute-done((f32[128,64,128]{2,1,0:T(8,128)}, f32[128,64,128]{2,1,0:T(8,128)}, u32[]{:S(2)}, u32[]{:S(2)}) %collective-permute-start) | collective-permute-done | bytes 4194336 | tf_op jit(solution)/shard_map/while/body/eval_jaxpr/ppermute | solution.py:42
  842.5 49.1 %collective-permute-done = f32[128,64,128]{2,1,0:T(8,128)} collective-permute-done((f32[128,64,128]{2,1,0:T(8,128)}, f32[128,64,128]{2,1,0:T(8,128)}, u32[]{:S(2)}, u32[]{:S(2)}) %collective-permute-start) | collective-permute-done | bytes 4194336 | tf_op jit(solution)/shard_map/while/body/eval_jaxpr/ppermute | solution.py:42
  899.5 49.1 %collective-permute-done = f32[128,64,128]{2,1,0:T(8,128)} collective-permute-done((f32[128,64,128]{2,1,0:T(8,128)}, f32[128,64,128]{2,1,0:T(8,128)}, u32[]{:S(2)}, u32[]{:S(2)}) %collective-permute-start) | collective-permute-done | bytes 4194336 | tf_op jit(solution)/shard_map/while/body/eval_jaxpr/ppermute | solution.py:42
  956.5 49.1 %collective-permute-done = f32[128,64,128]{2,1,0:T(8,128)} collective-permute-done((f32[128,64,128]{2,1,0:T(8,128)}, f32[128,64,128]{2,1,0:T(8,128)}, u32[]{:S(2)}, u32[]{:S(2)}) %collective-permute-start) | collective-permute-done | bytes 4194336 | tf_op jit(solution)/shard_map/while/body/eval_jaxpr/ppermute | solution.py:42
  1013.5 49.1 %collective-permute-done = f32[128,64,128]{2,1,0:T(8,128)} collective-permute-done((f32[128,64,128]{2,1,0:T(8,128)}, f32[128,64,128]{2,1,0:T(8,128)}, u32[]{:S(2)}, u32[]{:S(2)}) %collective-permute-start) | collective-permute-done | bytes 4194336 | tf_op jit(solution)/shard_map/while/body/eval_jaxpr/ppermute | solution.py:42
  1070.5 49.1 %collective-permute-done = f32[128,64,128]{2,1,0:T(8,128)} collective-permute-done((f32[128,64,128]{2,1,0:T(8,128)}, f32[128,64,128]{2,1,0:T(8,128)}, u32[]{:S(2)}, u32[]{:S(2)}) %collective-permute-start) | collective-permute-done | bytes 4194336 | tf_op jit(solution)/shard_map/while/body/eval_jaxpr/ppermute | solution.py:42
  1119.6 6.8 copy.28
  1134.4 69.1 %pad.29 = f32[4,128,64,128]{3,1,2,0:T(8,128)} pad(f32[2,128,64,128]{3,1,2,0:T(8,128)} %pad_maximum_fusion, f32[]{:T(128)} %constant.8.clone.1), padding=0_1_1x0_0_0x0_0_0x0_0_0 | pad | bytes 25165828 | tf_op jit(solution)/shard_map/pad | solution.py:37
  1203.5 69.1 %pad.30 = f32[4,128,64,128]{3,1,2,0:T(8,128)} pad(f32[2,128,64,128]{3,1,2,0:T(8,128)} %pad_add_fusion, f32[]{:T(128)} %constant.8.clone.1), padding=1_0_1x0_0_0x0_0_0x0_0_0 | pad | bytes 25165828 | tf_op jit(solution)/shard_map/pad | solution.py:37
  1272.6 9.4 slice_add_fusion
  1285.0 12.2 fusion.17
  1297.8 18.9 %fusion.2 = f32[4,128,128,64]{1,3,2,0:T(8,128)} fusion(bf16[4,128,128,64]{1,3,2,0:T(8,128)(2,1)} %copy.23, f32[4,128,128,64]{1,3,2,0:T(8,128)} %fusion.17, f32[4,128,128]{1,2,0:T(8,128)S(1)} %copy.22, f32[4,128,128]{1,2,0:T(8,128)S(1)} %copy.20, f32[4,128,128]{2,1,0:T(8,128)S(1)} %fusion.33, pred[128,128]{1,0:T(8,128)(4,1)S(1)} %iota_compare_fusion, ...), kind=kOutput, calls=%fused_computation.9 | convolution fusion | flops 1145044992 | bytes 43008512 | tf_op jit(solution)/shard_map/ctsh,cshp->cthp/dot_general | solution.py:51
  1316.7 30.4 %copy.37 = f32[4,128,128,64]{3,2,1,0:T(8,128)} copy(f32[4,128,128,64]{1,3,2,0:T(8,128)} %fusion.2) | data formatting | bytes 33554432 | tf_op jit(solution)/shard_map/reshape | solution.py:54
  1347.2 27.9 %reshape.84 = f32[512,8192]{1,0:T(8,128)} reshape(f32[4,128,128,64]{3,2,1,0:T(8,128)} %copy.37) | data formatting | bytes 33554432 | tf_op jit(solution)/shard_map/reshape | solution.py:54
  1375.1 50.7 %add_convert_fusion.1 = bf16[512,4096]{1,0:T(8,128)(2,1)} fusion(bf16[512,4096]{1,0:T(8,128)(2,1)} %param.8, bf16[8192,4096]{1,0:T(8,128)(2,1)} %param.13, f32[512,8192]{1,0:T(8,128)} %reshape.84, bf16[512,16768]{1,0:T(8,128)(2,1)} %convolution_convert_fusion), kind=kOutput, calls=%fused_computation.34 | convolution fusion | flops 34395389952 | bytes 100663296 | tf_op jit(solution)/shard_map/dot_general | solution.py:55
  (79 shorter events, 157.0 us)
Async XLA Ops:
  0.0 80.4 %copy-start.5 = (f32[128]{0:T(128)S(1)}, f32[128]{0:T(128)}, u32[]{:S(2)}) copy-start(f32[128]{0:T(128)} %param.11) | copy-start | bytes 1540
  0.0 81.5 %copy-start.6 = (f32[128]{0:T(128)S(1)}, f32[128]{0:T(128)}, u32[]{:S(2)}) copy-start(f32[128]{0:T(128)} %param.10) | copy-start | bytes 1540
  180.3 2.0 copy-start
  180.3 3.3 copy-start.2
  270.8 51.1 %collective-permute-start = (f32[128,64,128]{2,1,0:T(8,128)}, f32[128,64,128]{2,1,0:T(8,128)}, u32[]{:S(2)}, u32[]{:S(2)}) collective-permute-start(f32[128,64,128]{2,1,0:T(8,128)} %multiply_add_fusion.2), channel_id=1, source_target_pairs={{0,1},{1,2},{2,3},{3,4},{4,5},{5,6},{6,7},{7,8},{8,9},{9,10},{10,1... | collective-permute-start | bytes 12582920 | tf_op jit(solution)/shard_map/while/body/eval_jaxpr/ppermute | solution.py:42
  327.8 51.1 %collective-permute-start = (f32[128,64,128]{2,1,0:T(8,128)}, f32[128,64,128]{2,1,0:T(8,128)}, u32[]{:S(2)}, u32[]{:S(2)}) collective-permute-start(f32[128,64,128]{2,1,0:T(8,128)} %multiply_add_fusion.2), channel_id=1, source_target_pairs={{0,1},{1,2},{2,3},{3,4},{4,5},{5,6},{6,7},{7,8},{8,9},{9,10},{10,1... | collective-permute-start | bytes 12582920 | tf_op jit(solution)/shard_map/while/body/eval_jaxpr/ppermute | solution.py:42
  384.7 51.1 %collective-permute-start = (f32[128,64,128]{2,1,0:T(8,128)}, f32[128,64,128]{2,1,0:T(8,128)}, u32[]{:S(2)}, u32[]{:S(2)}) collective-permute-start(f32[128,64,128]{2,1,0:T(8,128)} %multiply_add_fusion.2), channel_id=1, source_target_pairs={{0,1},{1,2},{2,3},{3,4},{4,5},{5,6},{6,7},{7,8},{8,9},{9,10},{10,1... | collective-permute-start | bytes 12582920 | tf_op jit(solution)/shard_map/while/body/eval_jaxpr/ppermute | solution.py:42
  441.7 51.1 %collective-permute-start = (f32[128,64,128]{2,1,0:T(8,128)}, f32[128,64,128]{2,1,0:T(8,128)}, u32[]{:S(2)}, u32[]{:S(2)}) collective-permute-start(f32[128,64,128]{2,1,0:T(8,128)} %multiply_add_fusion.2), channel_id=1, source_target_pairs={{0,1},{1,2},{2,3},{3,4},{4,5},{5,6},{6,7},{7,8},{8,9},{9,10},{10,1... | collective-permute-start | bytes 12582920 | tf_op jit(solution)/shard_map/while/body/eval_jaxpr/ppermute | solution.py:42
  498.7 51.1 %collective-permute-start = (f32[128,64,128]{2,1,0:T(8,128)}, f32[128,64,128]{2,1,0:T(8,128)}, u32[]{:S(2)}, u32[]{:S(2)}) collective-permute-start(f32[128,64,128]{2,1,0:T(8,128)} %multiply_add_fusion.2), channel_id=1, source_target_pairs={{0,1},{1,2},{2,3},{3,4},{4,5},{5,6},{6,7},{7,8},{8,9},{9,10},{10,1... | collective-permute-start | bytes 12582920 | tf_op jit(solution)/shard_map/while/body/eval_jaxpr/ppermute | solution.py:42
  555.7 51.1 %collective-permute-start = (f32[128,64,128]{2,1,0:T(8,128)}, f32[128,64,128]{2,1,0:T(8,128)}, u32[]{:S(2)}, u32[]{:S(2)}) collective-permute-start(f32[128,64,128]{2,1,0:T(8,128)} %multiply_add_fusion.2), channel_id=1, source_target_pairs={{0,1},{1,2},{2,3},{3,4},{4,5},{5,6},{6,7},{7,8},{8,9},{9,10},{10,1... | collective-permute-start | bytes 12582920 | tf_op jit(solution)/shard_map/while/body/eval_jaxpr/ppermute | solution.py:42
  612.7 51.1 %collective-permute-start = (f32[128,64,128]{2,1,0:T(8,128)}, f32[128,64,128]{2,1,0:T(8,128)}, u32[]{:S(2)}, u32[]{:S(2)}) collective-permute-start(f32[128,64,128]{2,1,0:T(8,128)} %multiply_add_fusion.2), channel_id=1, source_target_pairs={{0,1},{1,2},{2,3},{3,4},{4,5},{5,6},{6,7},{7,8},{8,9},{9,10},{10,1... | collective-permute-start | bytes 12582920 | tf_op jit(solution)/shard_map/while/body/eval_jaxpr/ppermute | solution.py:42
  669.6 51.1 %collective-permute-start = (f32[128,64,128]{2,1,0:T(8,128)}, f32[128,64,128]{2,1,0:T(8,128)}, u32[]{:S(2)}, u32[]{:S(2)}) collective-permute-start(f32[128,64,128]{2,1,0:T(8,128)} %multiply_add_fusion.2), channel_id=1, source_target_pairs={{0,1},{1,2},{2,3},{3,4},{4,5},{5,6},{6,7},{7,8},{8,9},{9,10},{10,1... | collective-permute-start | bytes 12582920 | tf_op jit(solution)/shard_map/while/body/eval_jaxpr/ppermute | solution.py:42
  726.6 51.1 %collective-permute-start = (f32[128,64,128]{2,1,0:T(8,128)}, f32[128,64,128]{2,1,0:T(8,128)}, u32[]{:S(2)}, u32[]{:S(2)}) collective-permute-start(f32[128,64,128]{2,1,0:T(8,128)} %multiply_add_fusion.2), channel_id=1, source_target_pairs={{0,1},{1,2},{2,3},{3,4},{4,5},{5,6},{6,7},{7,8},{8,9},{9,10},{10,1... | collective-permute-start | bytes 12582920 | tf_op jit(solution)/shard_map/while/body/eval_jaxpr/ppermute | solution.py:42
  783.6 51.1 %collective-permute-start = (f32[128,64,128]{2,1,0:T(8,128)}, f32[128,64,128]{2,1,0:T(8,128)}, u32[]{:S(2)}, u32[]{:S(2)}) collective-permute-start(f32[128,64,128]{2,1,0:T(8,128)} %multiply_add_fusion.2), channel_id=1, source_target_pairs={{0,1},{1,2},{2,3},{3,4},{4,5},{5,6},{6,7},{7,8},{8,9},{9,10},{10,1... | collective-permute-start | bytes 12582920 | tf_op jit(solution)/shard_map/while/body/eval_jaxpr/ppermute | solution.py:42
  840.6 51.1 %collective-permute-start = (f32[128,64,128]{2,1,0:T(8,128)}, f32[128,64,128]{2,1,0:T(8,128)}, u32[]{:S(2)}, u32[]{:S(2)}) collective-permute-start(f32[128,64,128]{2,1,0:T(8,128)} %multiply_add_fusion.2), channel_id=1, source_target_pairs={{0,1},{1,2},{2,3},{3,4},{4,5},{5,6},{6,7},{7,8},{8,9},{9,10},{10,1... | collective-permute-start | bytes 12582920 | tf_op jit(solution)/shard_map/while/body/eval_jaxpr/ppermute | solution.py:42
  897.6 51.1 %collective-permute-start = (f32[128,64,128]{2,1,0:T(8,128)}, f32[128,64,128]{2,1,0:T(8,128)}, u32[]{:S(2)}, u32[]{:S(2)}) collective-permute-start(f32[128,64,128]{2,1,0:T(8,128)} %multiply_add_fusion.2), channel_id=1, source_target_pairs={{0,1},{1,2},{2,3},{3,4},{4,5},{5,6},{6,7},{7,8},{8,9},{9,10},{10,1... | collective-permute-start | bytes 12582920 | tf_op jit(solution)/shard_map/while/body/eval_jaxpr/ppermute | solution.py:42
  954.6 51.1 %collective-permute-start = (f32[128,64,128]{2,1,0:T(8,128)}, f32[128,64,128]{2,1,0:T(8,128)}, u32[]{:S(2)}, u32[]{:S(2)}) collective-permute-start(f32[128,64,128]{2,1,0:T(8,128)} %multiply_add_fusion.2), channel_id=1, source_target_pairs={{0,1},{1,2},{2,3},{3,4},{4,5},{5,6},{6,7},{7,8},{8,9},{9,10},{10,1... | collective-permute-start | bytes 12582920 | tf_op jit(solution)/shard_map/while/body/eval_jaxpr/ppermute | solution.py:42
  1011.5 51.1 %collective-permute-start = (f32[128,64,128]{2,1,0:T(8,128)}, f32[128,64,128]{2,1,0:T(8,128)}, u32[]{:S(2)}, u32[]{:S(2)}) collective-permute-start(f32[128,64,128]{2,1,0:T(8,128)} %multiply_add_fusion.2), channel_id=1, source_target_pairs={{0,1},{1,2},{2,3},{3,4},{4,5},{5,6},{6,7},{7,8},{8,9},{9,10},{10,1... | collective-permute-start | bytes 12582920 | tf_op jit(solution)/shard_map/while/body/eval_jaxpr/ppermute | solution.py:42
  1068.5 51.1 %collective-permute-start = (f32[128,64,128]{2,1,0:T(8,128)}, f32[128,64,128]{2,1,0:T(8,128)}, u32[]{:S(2)}, u32[]{:S(2)}) collective-permute-start(f32[128,64,128]{2,1,0:T(8,128)} %multiply_add_fusion.2), channel_id=1, source_target_pairs={{0,1},{1,2},{2,3},{3,4},{4,5},{5,6},{6,7},{7,8},{8,9},{9,10},{10,1... | collective-permute-start | bytes 12582920 | tf_op jit(solution)/shard_map/while/body/eval_jaxpr/ppermute | solution.py:42
  1119.6 6.8 copy-start.1
  1119.6 6.8 copy-start.3
  1272.6 9.4 copy-start.4
  1285.0 12.8 copy-start.7
where the time goes:
time: 1450 us; the launch traced here: 1430 us
  waiting for transfers between devices  737 us (51%)
  local copies, waits for them, and re-layouts  336 us (23%)
  matrix products  188 us (13%)
  other arithmetic  135 us (9%)
  starting transfers between devices  29.1 us (2%)
    ppermute x15, waiting for transfers between devices, pass_state(): return lax.ppermute(block_decay * carry + s_block, 'sp', hop_pairs)  737 us
    pad x4, local copies, waits for them, and re-layouts, local_mixer(): lax.associative_scan(combine_states, (seg_log, s_seg), axis=0)  138 us
    add x15, other arithmetic, pass_state(): return lax.ppermute(block_decay * carry + s_block, 'sp', hop_pairs)  88.9 us
    dot_general x1, matrix products, local_mixer(): jnp.dot(x_loc, w_in, preferred_element_type=jnp.float32)  80.4 us
    unnamed x17, local copies, waits for them, and re-layouts  71.4 us
    reshape x2, local copies, waits for them, and re-layouts, local_mixer(): y_all.reshape(tokens, inner) * jax.nn.silu(z_gate.astype(jnp.float32))  58.3 us
    dot_general x1, matrix products, local_mixer(): jnp.dot(gated, w_out, preferred_element_type=jnp.float32)  50.7 us
    reshape x2, local copies, waits for them, and re-layouts, local_mixer(): projected[:, inner:2 * inner].reshape(seg_count, SEG_LEN, heads, head_dim)  45.6 us
  transfers between devices with their start and end apart: 15, of which 15 were waited for; matrix products, arithmetic and copies ran while one was open for 0% of the time, Pallas kernels for 0%

commit v1 on v0

v1 whole, which is shorter than its diff:
```python
import functools

import jax
import jax.numpy as jnp
from jax import lax
from jax.experimental import pallas as pl
from jax.experimental.pallas import tpu as pltpu
from jax.sharding import PartitionSpec as P

SEG_LEN = 128
LANES = 128
CHUNK = 512
MASKED = -1e30


def mixer_kernel(seq_devs, x_hbm, w_in, a_neg, dt_bias, d_skip, w_out, out_hbm,
                 x_buf, win_buf, wout_buf, xs_buf, z_buf, acc, s_buf, h_buf, gated_a, gated_b,
                 c_buf, bt_buf, cb_buf, log_buf, q_buf, w1_buf, row_buf,
                 x_sem, win_sem, wout_sem, out_sem, send_sem, recv_sem):
    f32, bf16 = jnp.float32, jnp.bfloat16
    tokens, d_model = x_buf.shape
    inner = xs_buf.shape[1]
    heads = a_neg.shape[1]
    head_dim = inner // heads
    state = c_buf.shape[1]
    chunks = inner // CHUNK
    segs = tokens // SEG_LEN
    heads_chunk = CHUNK // head_dim
    small = 2 * state + heads
    n_tile = min(CHUNK, d_model)
    me = lax.axis_index("sp")
    right = lax.rem(me + 1, seq_devs)
    left = lax.rem(me + seq_devs - 1, seq_devs)
    delay = 4 * (me // 2) + lax.rem(me, 2)

    barrier = pltpu.get_barrier_semaphore()
    for peer in (left, right):
        pl.semaphore_signal(barrier, inc=1, device_id={"sp": peer}, device_id_type=pl.DeviceIdType.MESH)

    def small_copy():
        return pltpu.make_async_copy(w_in.at[:, pl.ds(2 * inner, small)], win_buf.at[0, :, pl.ds(0, small)], win_sem.at[0])

    def win_copy(step):
        column = jnp.where(step <= chunks, inner + CHUNK * (step - 1), CHUNK * (step - 1 - chunks))
        column = pl.multiple_of(column, CHUNK)
        slot = lax.rem(step, 2)
        return pltpu.make_async_copy(w_in.at[:, pl.ds(column, CHUNK)], win_buf.at[slot], win_sem.at[slot])

    def wout_copy(chunk):
        slot = lax.rem(chunk, 2)
        row = pl.multiple_of(CHUNK * chunk, CHUNK)
        return pltpu.make_async_copy(w_out.at[pl.ds(row, CHUNK), :], wout_buf.at[slot], wout_sem.at[slot])

    def state_copy(chunk):
        return pltpu.make_async_remote_copy(
            src_ref=s_buf.at[chunk], dst_ref=h_buf.at[chunk], send_sem=send_sem.at[chunk], recv_sem=recv_sem.at[chunk],
            device_id={"sp": right}, device_id_type=pl.DeviceIdType.MESH)

    x_copy = pltpu.make_async_copy(x_hbm, x_buf, x_sem)
    x_copy.start()
    small_copy().start()
    win_copy(jnp.int32(1)).start()

    @pl.when(me == 0)
    def _():
        def clear(chunk, carry):
            h_buf[chunk] = jnp.zeros(h_buf.shape[1:], f32)
            return carry
        lax.fori_loop(0, chunks, clear, 0)

    x_copy.wait()
    small_copy().wait()

    proj = jnp.dot(x_buf[...], win_buf[0, :, :small], preferred_element_type=f32).astype(bf16)
    c_buf[...] = proj[:, state:2 * state]
    bt_buf[...] = proj[:, :state].astype(f32).T.astype(bf16)
    dt = jax.nn.softplus(proj[:, 2 * state:].astype(f32) + dt_bias[...])
    logs = dt * a_neg[...]
    log_dt = jnp.log(dt)
    row_i = lax.broadcasted_iota(jnp.int32, (SEG_LEN, SEG_LEN), 0)
    col_i = lax.broadcasted_iota(jnp.int32, (SEG_LEN, SEG_LEN), 1)
    tri = jnp.where(row_i >= col_i, 1.0, 0.0).astype(f32)
    total = jnp.zeros((1, heads), f32)
    for seg in range(segs):
        rows = slice(SEG_LEN * seg, SEG_LEN * (seg + 1))
        cum = jnp.dot(tri, logs[rows], preferred_element_type=f32, precision=lax.Precision.HIGHEST)
        last = cum[SEG_LEN - 1:]
        log_buf[rows, :] = cum
        q_buf[:, rows] = (cum - log_dt[rows]).T
        w1_buf[rows, :] = jnp.exp(last - cum) * dt[rows]
        row_buf[seg:seg + 1, :] = jnp.exp(last)
        total = total + last
        cb_buf[rows, :] = jnp.dot(c_buf[rows, :], bt_buf[:, rows], preferred_element_type=f32)
    row_buf[segs:segs + 1, :] = jnp.exp(total)
    row_buf[segs + 1:segs + 2, :] = d_skip[...]
    row_buf[segs + 2:8, :] = jnp.zeros((8 - segs - 2, heads), f32)

    def low_half(rows):
        return lax.broadcasted_iota(jnp.int32, (rows, LANES), 1) < head_dim

    def chunk_heads(values, chunk):
        return pltpu.roll(values, lax.rem(heads - heads_chunk * chunk, heads), 1)

    def spread(rolled, pair):
        rows = rolled.shape[0]
        one = jnp.broadcast_to(rolled[:, 2 * pair:2 * pair + 1], (rows, LANES))
        two = jnp.broadcast_to(rolled[:, 2 * pair + 1:2 * pair + 2], (rows, LANES))
        return jnp.where(low_half(rows), one, two)

    def spread_rows(chunk):
        rolled = chunk_heads(row_buf[...], chunk)
        return jnp.concatenate([spread(rolled, pair) for pair in range(heads_chunk // 2)], axis=1)

    def columns_of(chunk):
        return pl.ds(pl.multiple_of(CHUNK * chunk, CHUNK), CHUNK)

    def seg_state(chunk, seg):
        rows = slice(SEG_LEN * seg, SEG_LEN * (seg + 1))
        rolled = chunk_heads(w1_buf[rows, :], chunk)
        factor = jnp.concatenate([spread(rolled, pair) for pair in range(heads_chunk // 2)], axis=1)
        weighted = (xs_buf[rows, columns_of(chunk)].astype(f32) * factor).astype(bf16)
        return jnp.dot(bt_buf[:, rows], weighted, preferred_element_type=f32)

    def block_state(chunk):
        decay = spread_rows(chunk)
        total_state = seg_state(chunk, 0)
        for seg in range(1, segs):
            total_state = decay[seg:seg + 1] * total_state + seg_state(chunk, seg)
        s_buf[chunk] = total_state

    def relay(step):
        chunk = step - 3 - delay

        @pl.when((chunk >= 0) & (chunk < chunks))
        def _():
            @pl.when(me > 0)
            def _():
                state_copy(chunk).wait_recv()

            @pl.when(me < seq_devs - 1)
            def _():
                decay = spread_rows(chunk)[segs:segs + 1]
                s_buf[chunk] = decay * h_buf[chunk] + s_buf[chunk]

    def forward(step):
        chunk = step - 3 - delay

        @pl.when((chunk >= 0) & (chunk < chunks) & (me < seq_devs - 1))
        def _():
            state_copy(chunk).start()

    def project(step, target, chunk):
        slot = lax.rem(step, 2)
        target[:, columns_of(chunk)] = jnp.dot(
            x_buf[...], win_buf[slot], preferred_element_type=f32).astype(bf16)

    def ssd(chunk, gated):
        columns = columns_of(chunk)
        table = spread_rows(chunk)
        state_now = h_buf[chunk]
        causal = row_i >= col_i
        low = low_half(SEG_LEN)
        for seg in range(segs):
            rows = slice(SEG_LEN * seg, SEG_LEN * (seg + 1))
            y_state = jnp.dot(c_buf[rows, :], state_now.astype(bf16), preferred_element_type=f32)
            rolled = chunk_heads(log_buf[rows, :], chunk)
            q_rows = q_buf[pl.ds(pl.multiple_of(heads_chunk * chunk, heads_chunk), heads_chunk), rows]
            x_seg = xs_buf[rows, columns]
            z_seg = z_buf[rows, columns]
            scores = cb_buf[rows, :]
            for pair in range(heads_chunk // 2):
                lanes = slice(LANES * pair, LANES * (pair + 1))
                logs_pair, mats = [], []
                for head in (2 * pair, 2 * pair + 1):
                    log_t = jnp.broadcast_to(rolled[:, head:head + 1], (SEG_LEN, SEG_LEN))
                    expo = jnp.where(causal, log_t - q_rows[head:head + 1, :], MASKED)
                    mats.append((scores * jnp.exp(expo)).astype(bf16))
                    logs_pair.append(log_t)
                x_pair = x_seg[:, lanes]
                nil = jnp.zeros_like(x_pair)
                rhs = jnp.concatenate([jnp.where(low, x_pair, nil), jnp.where(low, nil, x_pair)], axis=0)
                y_pair = jnp.dot(jnp.concatenate(mats, axis=1), rhs, preferred_element_type=f32)
                y_pair = y_pair + y_state[:, lanes] * jnp.exp(jnp.where(low, logs_pair[0], logs_pair[1]))
                y_pair = y_pair + table[segs + 1:segs + 2, lanes] * x_pair.astype(f32)
                z_pair = z_seg[:, lanes].astype(f32)
                gated[rows, lanes] = (y_pair * (z_pair / (1.0 + jnp.exp(-z_pair)))).astype(bf16)
            if seg < segs - 1:
                state_now = table[seg:seg + 1] * state_now + seg_state(chunk, seg)

    def accumulate(chunk, gated):
        slot = lax.rem(chunk, 2)
        acc[...] += jnp.dot(gated[...], wout_buf[slot], preferred_element_type=f32)

    win_copy(jnp.int32(1)).wait()
    win_copy(jnp.int32(2)).start()
    project(jnp.int32(1), xs_buf, jnp.int32(0))
    pl.semaphore_wait(barrier, 2)

    def xs_step(step, carry):
        relay(step)
        win_copy(step).wait()
        win_copy(step + 1).start()
        forward(step)
        block_state(step - 2)
        project(step, xs_buf, step - 1)
        return carry

    lax.fori_loop(2, chunks + 1, xs_step, 0)
    block_state(jnp.int32(chunks - 1))
    wout_copy(jnp.int32(0)).start()
    wout_copy(jnp.int32(1)).start()

    def z_step(step, carry):
        relay(step)
        win_copy(step).wait()

        @pl.when(step < 2 * chunks)
        def _():
            win_copy(step + 1).start()

        forward(step)
        chunk = step - 1 - chunks
        cleared = d_model // chunks
        acc[:, pl.ds(pl.multiple_of(cleared * chunk, cleared), cleared)] = jnp.zeros((tokens, cleared), f32)
        project(step, z_buf, chunk)
        return carry

    lax.fori_loop(chunks + 1, 2 * chunks + 1, z_step, 0)

    def mix(chunk, gated):
        step = 2 * chunks + 1 + chunk
        relay(step)
        forward(step)
        ssd(chunk, gated)

    def add_product(chunk, gated):
        wout_copy(chunk).wait()
        accumulate(chunk, gated)

        @pl.when(chunk + 2 < chunks)
        def _():
            wout_copy(chunk + 2).start()

    mix(jnp.int32(0), gated_a)

    def out_step(pair, carry):
        mix(2 * pair + 1, gated_b)
        add_product(2 * pair, gated_a)
        mix(2 * pair + 2, gated_a)
        add_product(2 * pair + 1, gated_b)
        return carry

    lax.fori_loop(0, chunks // 2 - 1, out_step, 0)
    mix(jnp.int32(chunks - 1), gated_b)
    add_product(jnp.int32(chunks - 2), gated_a)
    final = jnp.int32(chunks - 1)
    wout_copy(final).wait()

    def out_copy(tile):
        cols = pl.ds(n_tile * tile, n_tile)
        return pltpu.make_async_copy(x_buf.at[:, cols], out_hbm.at[:, cols], out_sem.at[tile])

    for tile in range(d_model // n_tile):
        cols = slice(n_tile * tile, n_tile * (tile + 1))
        product = jnp.dot(gated_b[...], wout_buf[(chunks - 1) % 2, :, cols], preferred_element_type=f32)
        x_buf[:, cols] = (x_buf[:, cols].astype(f32) + (acc[:, cols] + product)).astype(bf16)
        out_copy(tile).start()
    for tile in range(d_model // n_tile):
        out_copy(tile).wait()

    @pl.when(me < seq_devs - 1)
    def _():
        def drain(chunk, carry):
            state_copy(chunk).wait_send()
            return carry
        lax.fori_loop(0, chunks, drain, 0)


def solution(mesh):
    seq_devs = mesh.shape["sp"]
    row_spec = P(("dp", "sp"), None)

    def local_mixer(x_loc, w_in, a_neg, dt_bias, d_skip, w_out):
        f32, bf16 = jnp.float32, jnp.bfloat16
        tokens, d_model = x_loc.shape
        inner = w_out.shape[0]
        heads = a_neg.shape[0]
        state = (w_in.shape[1] - 2 * inner - heads) // 2
        chunks = inner // CHUNK
        any_spec = pl.BlockSpec(memory_space=pl.ANY)
        vmem_spec = pl.BlockSpec(memory_space=pltpu.VMEM)
        return pl.pallas_call(
            functools.partial(mixer_kernel, seq_devs),
            out_shape=jax.ShapeDtypeStruct((tokens, d_model), bf16),
            in_specs=[any_spec, any_spec, vmem_spec, vmem_spec, vmem_spec, any_spec],
            out_specs=any_spec,
            scratch_shapes=[
                pltpu.VMEM((tokens, d_model), bf16),
                pltpu.VMEM((2, d_model, CHUNK), bf16),
                pltpu.VMEM((2, CHUNK, d_model), bf16),
                pltpu.VMEM((tokens, inner), bf16),
                pltpu.VMEM((tokens, inner), bf16),
                pltpu.VMEM((tokens, d_model), f32),
                pltpu.VMEM((chunks, state, CHUNK), f32),
                pltpu.VMEM((chunks, state, CHUNK), f32),
                pltpu.VMEM((tokens, CHUNK), bf16),
                pltpu.VMEM((tokens, CHUNK), bf16),
                pltpu.VMEM((tokens, state), bf16),
                pltpu.VMEM((state, tokens), bf16),
                pltpu.VMEM((tokens, SEG_LEN), f32),
                pltpu.VMEM((tokens, heads), f32),
                pltpu.VMEM((heads, tokens), f32),
                pltpu.VMEM((tokens, heads), f32),
                pltpu.VMEM((8, heads), f32),
                pltpu.SemaphoreType.DMA,
                pltpu.SemaphoreType.DMA((2,)),
                pltpu.SemaphoreType.DMA((2,)),
                pltpu.SemaphoreType.DMA((max(1, d_model // CHUNK),)),
                pltpu.SemaphoreType.DMA((chunks,)),
                pltpu.SemaphoreType.DMA((chunks,)),
            ],
            compiler_params=pltpu.CompilerParams(
                collective_id=0, has_side_effects=True, vmem_limit_bytes=67043328),
        )(x_loc, w_in, a_neg[None], dt_bias[None], d_skip[None], w_out)

    return jax.shard_map(local_mixer, mesh=mesh, in_specs=(row_spec, P(), P(), P(), P(), P()),
                         out_specs=row_spec, check_vma=False)
```

time: 1450 us -> 186 us (0.13)
  the two profiles are of different devices: /device:TPU:158 before, /device:TPU:21 now
where the time goes in v1:
time: 186 us; the launch traced here: 185 us
  Pallas kernels  181 us (97%)
  local copies, waits for them, and re-layouts  4.7 us (3%)
    pallas_call x1, Pallas kernels, local_mixer(): pl.pallas_call(functools.partial(mixer_kernel, seq_devs), out_shape=jax.S...  181 us
    unnamed x1, local copies, waits for them, and re-layouts  4.7 us

profile of v1, /device:TPU:21, one launch (start us, length us, event | category | flops | bytes accessed | tf_op | source)
XLA Modules:
  0.0 185.4 jit_solution(5585666697260541382)
XLA Ops:
  0.0 180.7 %shard_map.64 = bf16[512,4096]{1,0:T(8,128)(2,1)} custom-call(bf16[512,4096]{1,0:T(8,128)(2,1)} %x_hbm.1, bf16[4096,16768]{1,0:T(8,128)(2,1)} %w_in.1, f32[1,128]{1,0:T(1,128)} %bitcast.3, f32[1,128]{1,0:T(1,128)} %bitcast.4, f32[1,128]{1,0:T(1,128)} %bitcast.5, bf16[8192,4096]{1,0:T(8,128)(2,1)} %w_out.1), custom_call_target="tpu_custom_call" | custom-call | tf_op jit(solution)/shard_map/pallas_call | solution.py:292
  180.7 4.7 %copy.8 = bf16[512,4096]{1,0:T(8,128)(2,1)} copy(bf16[512,4096]{1,0:T(8,128)(2,1)} %shard_map.64) | data formatting | bytes 8388608

commit v2 on v1

--- a/solution.py
+++ b/solution.py
@@ -11,11 +11,12 @@
 LANES = 128
 CHUNK = 512
 MASKED = -1e30
+LOG2E = 1.4426950408889634
 
 
 def mixer_kernel(seq_devs, x_hbm, w_in, a_neg, dt_bias, d_skip, w_out, out_hbm,
                  x_buf, win_buf, wout_buf, xs_buf, z_buf, acc, s_buf, h_buf, gated_a, gated_b,
-                 c_buf, bt_buf, cb_buf, log_buf, q_buf, w1_buf, row_buf,
+                 xw_buf, c_buf, bt_buf, cb_buf, log_buf, q_buf, w1_buf, row_buf, decay_buf,
                  x_sem, win_sem, wout_sem, out_sem, send_sem, recv_sem):
     f32, bf16 = jnp.float32, jnp.bfloat16
     tokens, d_model = x_buf.shape
@@ -72,11 +73,14 @@
     small_copy().wait()
 
     proj = jnp.dot(x_buf[...], win_buf[0, :, :small], preferred_element_type=f32).astype(bf16)
+    win_copy(jnp.int32(1)).wait()
+    win_copy(jnp.int32(2)).start()
+    xs_buf[:, :CHUNK] = jnp.dot(x_buf[...], win_buf[1], preferred_element_type=f32).astype(bf16)
     c_buf[...] = proj[:, state:2 * state]
     bt_buf[...] = proj[:, :state].astype(f32).T.astype(bf16)
     dt = jax.nn.softplus(proj[:, 2 * state:].astype(f32) + dt_bias[...])
     logs = dt * a_neg[...]
-    log_dt = jnp.log(dt)
+    log_dt = jnp.log(dt) * LOG2E
     row_i = lax.broadcasted_iota(jnp.int32, (SEG_LEN, SEG_LEN), 0)
     col_i = lax.broadcasted_iota(jnp.int32, (SEG_LEN, SEG_LEN), 1)
     tri = jnp.where(row_i >= col_i, 1.0, 0.0).astype(f32)
@@ -85,8 +89,8 @@
         rows = slice(SEG_LEN * seg, SEG_LEN * (seg + 1))
         cum = jnp.dot(tri, logs[rows], preferred_element_type=f32, precision=lax.Precision.HIGHEST)
         last = cum[SEG_LEN - 1:]
-        log_buf[rows, :] = cum
-        q_buf[:, rows] = (cum - log_dt[rows]).T
+        log_buf[rows, :] = cum * LOG2E
+        q_buf[:, rows] = (cum * LOG2E - log_dt[rows]).T
         w1_buf[rows, :] = jnp.exp(last - cum) * dt[rows]
         row_buf[seg:seg + 1, :] = jnp.exp(last)
         total = total + last
@@ -99,6 +103,7 @@
         return lax.broadcasted_iota(jnp.int32, (rows, LANES), 1) < head_dim
 
     def chunk_heads(values, chunk):
+        chunk = jnp.int32(chunk)
         return pltpu.roll(values, lax.rem(heads - heads_chunk * chunk, heads), 1)
 
     def spread(rolled, pair):
@@ -112,20 +117,29 @@
         return jnp.concatenate([spread(rolled, pair) for pair in range(heads_chunk // 2)], axis=1)
 
     def columns_of(chunk):
+        if isinstance(chunk, int):
+            return slice(CHUNK * chunk, CHUNK * (chunk + 1))
         return pl.ds(pl.multiple_of(CHUNK * chunk, CHUNK), CHUNK)
 
-    def seg_state(chunk, seg):
+    def weigh(chunk, seg):
         rows = slice(SEG_LEN * seg, SEG_LEN * (seg + 1))
         rolled = chunk_heads(w1_buf[rows, :], chunk)
         factor = jnp.concatenate([spread(rolled, pair) for pair in range(heads_chunk // 2)], axis=1)
-        weighted = (xs_buf[rows, columns_of(chunk)].astype(f32) * factor).astype(bf16)
-        return jnp.dot(bt_buf[:, rows], weighted, preferred_element_type=f32)
+        return (xs_buf[rows, columns_of(chunk)].astype(f32) * factor).astype(bf16)
+
+    def seg_state(weighted, seg):
+        return jnp.dot(bt_buf[:, SEG_LEN * seg:SEG_LEN * (seg + 1)], weighted, preferred_element_type=f32)
+
+    def weigh_block(chunk):
+        decay_buf[chunk] = spread_rows(chunk)
+        for seg in range(segs):
+            xw_buf[SEG_LEN * seg:SEG_LEN * (seg + 1), :] = weigh(chunk, seg)
 
     def block_state(chunk):
-        decay = spread_rows(chunk)
-        total_state = seg_state(chunk, 0)
+        total_state = seg_state(xw_buf[:SEG_LEN, :], 0)
         for seg in range(1, segs):
-            total_state = decay[seg:seg + 1] * total_state + seg_state(chunk, seg)
+            total_state = (decay_buf[chunk, seg:seg + 1] * total_state
+                           + seg_state(xw_buf[SEG_LEN * seg:SEG_LEN * (seg + 1), :], seg))
         s_buf[chunk] = total_state
 
     def relay(step):
@@ -139,7 +153,7 @@
 
             @pl.when(me < seq_devs - 1)
             def _():
-                decay = spread_rows(chunk)[segs:segs + 1]
+                decay = decay_buf[chunk, segs:segs + 1]
                 s_buf[chunk] = decay * h_buf[chunk] + s_buf[chunk]
 
     def forward(step):
@@ -150,50 +164,51 @@
             state_copy(chunk).start()
 
     def project(step, target, chunk):
-        slot = lax.rem(step, 2)
+        slot = step % 2 if isinstance(step, int) else lax.rem(step, 2)
         target[:, columns_of(chunk)] = jnp.dot(
             x_buf[...], win_buf[slot], preferred_element_type=f32).astype(bf16)
 
-    def ssd(chunk, gated):
+    def ssd_seg(chunk, seg, state_now, gated):
         columns = columns_of(chunk)
-        table = spread_rows(chunk)
+        table = decay_buf.at[chunk]
+        low = low_half(SEG_LEN)
+        rows = slice(SEG_LEN * seg, SEG_LEN * (seg + 1))
+        y_state = jnp.dot(c_buf[rows, :], state_now.astype(bf16), preferred_element_type=f32)
+        rolled = chunk_heads(log_buf[rows, :], chunk)
+        first_head = heads_chunk * chunk
+        if not isinstance(chunk, int):
+            first_head = pl.multiple_of(first_head, heads_chunk)
+        q_rows = q_buf[pl.ds(first_head, heads_chunk), rows]
+        x_seg = xs_buf[rows, columns]
+        z_seg = z_buf[rows, columns]
+        scores = cb_buf[rows, :]
+        causal = row_i >= col_i
+        for pair in range(heads_chunk // 2):
+            lanes = slice(LANES * pair, LANES * (pair + 1))
+            logs_pair, mats = [], []
+            for head in (2 * pair, 2 * pair + 1):
+                log_t = jnp.broadcast_to(rolled[:, head:head + 1], (SEG_LEN, SEG_LEN))
+                expo = jnp.where(causal, log_t - q_rows[head:head + 1, :], MASKED)
+                mats.append((scores * jnp.exp2(expo)).astype(bf16))
+                logs_pair.append(log_t)
+            x_pair = x_seg[:, lanes]
+            nil = jnp.zeros_like(x_pair)
+            rhs = jnp.concatenate([jnp.where(low, x_pair, nil), jnp.where(low, nil, x_pair)], axis=0)
+            y_pair = jnp.dot(jnp.concatenate(mats, axis=1), rhs, preferred_element_type=f32)
+            y_pair = y_pair + y_state[:, lanes] * jnp.exp2(jnp.where(low, logs_pair[0], logs_pair[1]))
+            y_pair = y_pair + table[segs + 1:segs + 2, lanes] * x_pair.astype(f32)
+            z_pair = z_seg[:, lanes].astype(f32)
+            gated[rows, lanes] = (y_pair * (z_pair / (1.0 + jnp.exp2(z_pair * -LOG2E)))).astype(bf16)
+        if seg < segs - 1:
+            state_now = table[seg:seg + 1] * state_now + seg_state(weigh(chunk, seg), seg)
+        return state_now
+
+    def mix_and_add(chunk, gated, done, piece_of):
         state_now = h_buf[chunk]
-        causal = row_i >= col_i
-        low = low_half(SEG_LEN)
         for seg in range(segs):
-            rows = slice(SEG_LEN * seg, SEG_LEN * (seg + 1))
-            y_state = jnp.dot(c_buf[rows, :], state_now.astype(bf16), preferred_element_type=f32)
-            rolled = chunk_heads(log_buf[rows, :], chunk)
-            q_rows = q_buf[pl.ds(pl.multiple_of(heads_chunk * chunk, heads_chunk), heads_chunk), rows]
-            x_seg = xs_buf[rows, columns]
-            z_seg = z_buf[rows, columns]
-            scores = cb_buf[rows, :]
-            for pair in range(heads_chunk // 2):
-                lanes = slice(LANES * pair, LANES * (pair + 1))
-                logs_pair, mats = [], []
-                for head in (2 * pair, 2 * pair + 1):
-                    log_t = jnp.broadcast_to(rolled[:, head:head + 1], (SEG_LEN, SEG_LEN))
-                    expo = jnp.where(causal, log_t - q_rows[head:head + 1, :], MASKED)
-                    mats.append((scores * jnp.exp(expo)).astype(bf16))
-                    logs_pair.append(log_t)
-                x_pair = x_seg[:, lanes]
-                nil = jnp.zeros_like(x_pair)
-                rhs = jnp.concatenate([jnp.where(low, x_pair, nil), jnp.where(low, nil, x_pair)], axis=0)
-                y_pair = jnp.dot(jnp.concatenate(mats, axis=1), rhs, preferred_element_type=f32)
-                y_pair = y_pair + y_state[:, lanes] * jnp.exp(jnp.where(low, logs_pair[0], logs_pair[1]))
-                y_pair = y_pair + table[segs + 1:segs + 2, lanes] * x_pair.astype(f32)
-                z_pair = z_seg[:, lanes].astype(f32)
-                gated[rows, lanes] = (y_pair * (z_pair / (1.0 + jnp.exp(-z_pair)))).astype(bf16)
-            if seg < segs - 1:
-                state_now = table[seg:seg + 1] * state_now + seg_state(chunk, seg)
-
-    def accumulate(chunk, gated):
-        slot = lax.rem(chunk, 2)
-        acc[...] += jnp.dot(gated[...], wout_buf[slot], preferred_element_type=f32)
-
-    win_copy(jnp.int32(1)).wait()
-    win_copy(jnp.int32(2)).start()
-    project(jnp.int32(1), xs_buf, jnp.int32(0))
+            piece_of(seg)
+            state_now = ssd_seg(chunk, seg, state_now, gated)
+
     pl.semaphore_wait(barrier, 2)
 
     def xs_step(step, carry):
@@ -201,58 +216,70 @@
         win_copy(step).wait()
         win_copy(step + 1).start()
         forward(step)
+        weigh_block(step - 2)
+        project(step, xs_buf, step - 1)
         block_state(step - 2)
-        project(step, xs_buf, step - 1)
         return carry
 
     lax.fori_loop(2, chunks + 1, xs_step, 0)
-    block_state(jnp.int32(chunks - 1))
-    wout_copy(jnp.int32(0)).start()
-    wout_copy(jnp.int32(1)).start()
-
-    def z_step(step, carry):
+
+    def z_part(step, chunk):
+        cleared = d_model // chunks
+        start = cleared * chunk if isinstance(chunk, int) else pl.multiple_of(cleared * chunk, cleared)
+        acc[:, pl.ds(start, cleared)] = jnp.zeros((tokens, cleared), f32)
+        project(step, z_buf, chunk)
+
+    def z_enter(step):
+        step = jnp.int32(step)
         relay(step)
         win_copy(step).wait()
-
-        @pl.when(step < 2 * chunks)
-        def _():
-            win_copy(step + 1).start()
-
+        win_copy(step + 1).start()
         forward(step)
-        chunk = step - 1 - chunks
-        cleared = d_model // chunks
-        acc[:, pl.ds(pl.multiple_of(cleared * chunk, cleared), cleared)] = jnp.zeros((tokens, cleared), f32)
-        project(step, z_buf, chunk)
+
+    z_enter(chunks + 1)
+    weigh_block(chunks - 1)
+    z_part(chunks + 1, 0)
+    block_state(chunks - 1)
+    wout_copy(jnp.int32(0)).start()
+
+    def z_step(step, carry):
+        z_enter(step)
+        z_part(step, step - 1 - chunks)
         return carry
 
-    lax.fori_loop(chunks + 1, 2 * chunks + 1, z_step, 0)
-
-    def mix(chunk, gated):
-        step = 2 * chunks + 1 + chunk
+    lax.fori_loop(chunks + 2, 2 * chunks, z_step, 0)
+    last_z = jnp.int32(2 * chunks)
+    relay(last_z)
+    win_copy(last_z).wait()
+    forward(last_z)
+    z_pieces = [z_part] + [lambda step, chunk: None] * (segs - 1)
+    mix_and_add(0, gated_a, None, lambda seg: z_pieces[seg](2 * chunks, chunks - 1))
+
+    def out_part(chunk, gated, piece):
+        width = d_model // segs
+        cols = slice(width * piece, width * (piece + 1))
+        slot = chunk % 2 if isinstance(chunk, int) else lax.rem(chunk, 2)
+        acc[:, cols] += jnp.dot(gated[...], wout_buf[slot, :, cols], preferred_element_type=f32)
+
+    def out_enter(chunk):
+        chunk = jnp.int32(chunk)
+        step = 2 * chunks + chunk
         relay(step)
+        wout_copy(chunk - 1).wait()
+        wout_copy(chunk).start()
         forward(step)
-        ssd(chunk, gated)
-
-    def add_product(chunk, gated):
-        wout_copy(chunk).wait()
-        accumulate(chunk, gated)
-
-        @pl.when(chunk + 2 < chunks)
-        def _():
-            wout_copy(chunk + 2).start()
-
-    mix(jnp.int32(0), gated_a)
+
+    def out_chunk(chunk, gated, before):
+        out_enter(chunk)
+        mix_and_add(chunk, gated, before, lambda seg: out_part(chunk - 1, before, seg))
 
     def out_step(pair, carry):
-        mix(2 * pair + 1, gated_b)
-        add_product(2 * pair, gated_a)
-        mix(2 * pair + 2, gated_a)
-        add_product(2 * pair + 1, gated_b)
+        out_chunk(2 * pair + 1, gated_b, gated_a)
+        out_chunk(2 * pair + 2, gated_a, gated_b)
         return carry
 
     lax.fori_loop(0, chunks // 2 - 1, out_step, 0)
-    mix(jnp.int32(chunks - 1), gated_b)
-    add_product(jnp.int32(chunks - 2), gated_a)
+    out_chunk(chunks - 1, gated_b, gated_a)
     final = jnp.int32(chunks - 1)
     wout_copy(final).wait()
 
@@ -305,6 +332,7 @@
                 pltpu.VMEM((chunks, state, CHUNK), f32),
                 pltpu.VMEM((tokens, CHUNK), bf16),
                 pltpu.VMEM((tokens, CHUNK), bf16),
+                pltpu.VMEM((tokens, CHUNK), bf16),
                 pltpu.VMEM((tokens, state), bf16),
                 pltpu.VMEM((state, tokens), bf16),
                 pltpu.VMEM((tokens, SEG_LEN), f32),
@@ -312,6 +340,7 @@
                 pltpu.VMEM((heads, tokens), f32),
                 pltpu.VMEM((tokens, heads), f32),
                 pltpu.VMEM((8, heads), f32),
+                pltpu.VMEM((chunks, 8, CHUNK), f32),
                 pltpu.SemaphoreType.DMA,
                 pltpu.SemaphoreType.DMA((2,)),
                 pltpu.SemaphoreType.DMA((2,)),

time: 186 us -> 148 us (0.80)
  Pallas kernels: 181 us -> 143 us
    pallas_call x1, Pallas kernels: 181 us -> 143 us  [local_mixer(): pl.pallas_call(functools.partial(mixer_kernel, seq_devs), out_shape=jax.S...]
where the time goes in v2:
time: 148 us; the launch traced here: 147 us
  Pallas kernels  143 us (97%)
  local copies, waits for them, and re-layouts  4.7 us (3%)
    pallas_call x1, Pallas kernels, local_mixer(): pl.pallas_call(functools.partial(mixer_kernel, seq_devs), out_shape=jax.S...  143 us
    unnamed x1, local copies, waits for them, and re-layouts  4.7 us

profile of v2, /device:TPU:21, one launch (start us, length us, event | category | flops | bytes accessed | tf_op | source)
XLA Modules:
  0.0 147.3 jit_solution(6132781955760587604)
XLA Ops:
  0.0 142.6 %shard_map.64 = bf16[512,4096]{1,0:T(8,128)(2,1)} custom-call(bf16[512,4096]{1,0:T(8,128)(2,1)} %x_hbm.1, bf16[4096,16768]{1,0:T(8,128)(2,1)} %w_in.1, f32[1,128]{1,0:T(1,128)} %bitcast.3, f32[1,128]{1,0:T(1,128)} %bitcast.4, f32[1,128]{1,0:T(1,128)} %bitcast.5, bf16[8192,4096]{1,0:T(8,128)(2,1)} %w_out.1), custom_call_target="tpu_custom_call" | custom-call | tf_op jit(solution)/shard_map/pallas_call | solution.py:319
  142.6 4.7 %copy.8 = bf16[512,4096]{1,0:T(8,128)(2,1)} copy(bf16[512,4096]{1,0:T(8,128)(2,1)} %shard_map.64) | data formatting | bytes 8388608

commit v3 on v2

--- a/solution.py
+++ b/solution.py
@@ -10,16 +10,17 @@
 SEG_LEN = 128
 LANES = 128
 CHUNK = 512
+PIECES = 4
 MASKED = -1e30
 LOG2E = 1.4426950408889634
 
 
-def mixer_kernel(seq_devs, x_hbm, w_in, a_neg, dt_bias, d_skip, w_out, out_hbm,
-                 x_buf, win_buf, wout_buf, xs_buf, z_buf, acc, s_buf, h_buf, gated_a, gated_b,
+def mixer_kernel(seq_devs, x_hbm, w_in, a_neg, dt_bias, d_skip, w_out, out_ref,
+                 win_buf, wout_buf, xs_buf, z_buf, acc, s_buf, h_buf, gated_a, gated_b,
                  xw_buf, c_buf, bt_buf, cb_buf, log_buf, q_buf, w1_buf, row_buf, decay_buf,
-                 x_sem, win_sem, wout_sem, out_sem, send_sem, recv_sem):
+                 x_sem, small_sem, first_sem, win_sem, wout_sem, send_sem, recv_sem):
     f32, bf16 = jnp.float32, jnp.bfloat16
-    tokens, d_model = x_buf.shape
+    tokens, d_model = out_ref.shape
     inner = xs_buf.shape[1]
     heads = a_neg.shape[1]
     head_dim = inner // heads
@@ -28,7 +29,7 @@
     segs = tokens // SEG_LEN
     heads_chunk = CHUNK // head_dim
     small = 2 * state + heads
-    n_tile = min(CHUNK, d_model)
+    k_tile = d_model // PIECES
     me = lax.axis_index("sp")
     right = lax.rem(me + 1, seq_devs)
     left = lax.rem(me + seq_devs - 1, seq_devs)
@@ -38,8 +39,19 @@
     for peer in (left, right):
         pl.semaphore_signal(barrier, inc=1, device_id={"sp": peer}, device_id_type=pl.DeviceIdType.MESH)
 
-    def small_copy():
-        return pltpu.make_async_copy(w_in.at[:, pl.ds(2 * inner, small)], win_buf.at[0, :, pl.ds(0, small)], win_sem.at[0])
+    def x_copy(piece):
+        cols = pl.ds(k_tile * piece, k_tile)
+        return pltpu.make_async_copy(x_hbm.at[:, cols], out_ref.at[:, cols], x_sem.at[piece])
+
+    def small_copy(piece):
+        rows = pl.ds(k_tile * piece, k_tile)
+        return pltpu.make_async_copy(
+            w_in.at[rows, pl.ds(2 * inner, small)], win_buf.at[0, rows, pl.ds(0, small)], small_sem.at[piece])
+
+    def first_copy(piece):
+        rows = pl.ds(k_tile * piece, k_tile)
+        return pltpu.make_async_copy(
+            w_in.at[rows, pl.ds(inner, CHUNK)], win_buf.at[1, rows, :], first_sem.at[piece])
 
     def win_copy(step):
         column = jnp.where(step <= chunks, inner + CHUNK * (step - 1), CHUNK * (step - 1 - chunks))
@@ -57,10 +69,11 @@
             src_ref=s_buf.at[chunk], dst_ref=h_buf.at[chunk], send_sem=send_sem.at[chunk], recv_sem=recv_sem.at[chunk],
             device_id={"sp": right}, device_id_type=pl.DeviceIdType.MESH)
 
-    x_copy = pltpu.make_async_copy(x_hbm, x_buf, x_sem)
-    x_copy.start()
-    small_copy().start()
-    win_copy(jnp.int32(1)).start()
+    for piece in range(PIECES):
+        x_copy(piece).start()
+        small_copy(piece).start()
+    for piece in range(PIECES):
+        first_copy(piece).start()
 
     @pl.when(me == 0)
     def _():
@@ -69,13 +82,20 @@
             return carry
         lax.fori_loop(0, chunks, clear, 0)
 
-    x_copy.wait()
-    small_copy().wait()
-
-    proj = jnp.dot(x_buf[...], win_buf[0, :, :small], preferred_element_type=f32).astype(bf16)
-    win_copy(jnp.int32(1)).wait()
+    proj = jnp.zeros((tokens, small), f32)
+    for piece in range(PIECES):
+        x_copy(piece).wait()
+        small_copy(piece).wait()
+        part = slice(k_tile * piece, k_tile * (piece + 1))
+        proj = proj + jnp.dot(out_ref[:, part], win_buf[0, part, :small], preferred_element_type=f32)
+    proj = proj.astype(bf16)
     win_copy(jnp.int32(2)).start()
-    xs_buf[:, :CHUNK] = jnp.dot(x_buf[...], win_buf[1], preferred_element_type=f32).astype(bf16)
+    first = jnp.zeros((tokens, CHUNK), f32)
+    for piece in range(PIECES):
+        first_copy(piece).wait()
+        part = slice(k_tile * piece, k_tile * (piece + 1))
+        first = first + jnp.dot(out_ref[:, part], win_buf[1, part, :], preferred_element_type=f32)
+    xs_buf[:, :CHUNK] = first.astype(bf16)
     c_buf[...] = proj[:, state:2 * state]
     bt_buf[...] = proj[:, :state].astype(f32).T.astype(bf16)
     dt = jax.nn.softplus(proj[:, 2 * state:].astype(f32) + dt_bias[...])
@@ -166,7 +186,7 @@
     def project(step, target, chunk):
         slot = step % 2 if isinstance(step, int) else lax.rem(step, 2)
         target[:, columns_of(chunk)] = jnp.dot(
-            x_buf[...], win_buf[slot], preferred_element_type=f32).astype(bf16)
+            out_ref[...], win_buf[slot], preferred_element_type=f32).astype(bf16)
 
     def ssd_seg(chunk, seg, state_now, gated):
         columns = columns_of(chunk)
@@ -203,7 +223,7 @@
             state_now = table[seg:seg + 1] * state_now + seg_state(weigh(chunk, seg), seg)
         return state_now
 
-    def mix_and_add(chunk, gated, done, piece_of):
+    def mix_and_add(chunk, gated, piece_of):
         state_now = h_buf[chunk]
         for seg in range(segs):
             piece_of(seg)
@@ -252,8 +272,17 @@
     relay(last_z)
     win_copy(last_z).wait()
     forward(last_z)
-    z_pieces = [z_part] + [lambda step, chunk: None] * (segs - 1)
-    mix_and_add(0, gated_a, None, lambda seg: z_pieces[seg](2 * chunks, chunks - 1))
+    cleared = d_model // chunks
+    acc[:, cleared * (chunks - 1):] = jnp.zeros((tokens, cleared), f32)
+
+    def z_piece(seg):
+        if seg % 2 == 0:
+            width = 2 * CHUNK // segs
+            start = width * (seg // 2)
+            z_buf[:, inner - CHUNK + start:inner - CHUNK + start + width] = jnp.dot(
+                out_ref[...], win_buf[(2 * chunks) % 2, :, start:start + width], preferred_element_type=f32).astype(bf16)
+
+    mix_and_add(0, gated_a, z_piece)
 
     def out_part(chunk, gated, piece):
         width = d_model // segs
@@ -271,7 +300,7 @@
 
     def out_chunk(chunk, gated, before):
         out_enter(chunk)
-        mix_and_add(chunk, gated, before, lambda seg: out_part(chunk - 1, before, seg))
+        mix_and_add(chunk, gated, lambda seg: out_part(chunk - 1, before, seg))
 
     def out_step(pair, carry):
         out_chunk(2 * pair + 1, gated_b, gated_a)
@@ -283,17 +312,11 @@
     final = jnp.int32(chunks - 1)
     wout_copy(final).wait()
 
-    def out_copy(tile):
-        cols = pl.ds(n_tile * tile, n_tile)
-        return pltpu.make_async_copy(x_buf.at[:, cols], out_hbm.at[:, cols], out_sem.at[tile])
-
-    for tile in range(d_model // n_tile):
-        cols = slice(n_tile * tile, n_tile * (tile + 1))
+    width = d_model // segs
+    for piece in range(segs):
+        cols = slice(width * piece, width * (piece + 1))
         product = jnp.dot(gated_b[...], wout_buf[(chunks - 1) % 2, :, cols], preferred_element_type=f32)
-        x_buf[:, cols] = (x_buf[:, cols].astype(f32) + (acc[:, cols] + product)).astype(bf16)
-        out_copy(tile).start()
-    for tile in range(d_model // n_tile):
-        out_copy(tile).wait()
+        out_ref[:, cols] = (out_ref[:, cols].astype(f32) + (acc[:, cols] + product)).astype(bf16)
 
     @pl.when(me < seq_devs - 1)
     def _():
@@ -318,11 +341,10 @@
         vmem_spec = pl.BlockSpec(memory_space=pltpu.VMEM)
         return pl.pallas_call(
             functools.partial(mixer_kernel, seq_devs),
-            out_shape=jax.ShapeDtypeStruct((tokens, d_model), bf16),
+            out_shape=pltpu.VMEM((tokens, d_model), bf16),
             in_specs=[any_spec, any_spec, vmem_spec, vmem_spec, vmem_spec, any_spec],
-            out_specs=any_spec,
+            out_specs=vmem_spec,
             scratch_shapes=[
-                pltpu.VMEM((tokens, d_model), bf16),
                 pltpu.VMEM((2, d_model, CHUNK), bf16),
                 pltpu.VMEM((2, CHUNK, d_model), bf16),
                 pltpu.VMEM((tokens, inner), bf16),
@@ -341,15 +363,16 @@
                 pltpu.VMEM((tokens, heads), f32),
                 pltpu.VMEM((8, heads), f32),
                 pltpu.VMEM((chunks, 8, CHUNK), f32),
-                pltpu.SemaphoreType.DMA,
+                pltpu.SemaphoreType.DMA((PIECES,)),
+                pltpu.SemaphoreType.DMA((PIECES,)),
+                pltpu.SemaphoreType.DMA((PIECES,)),
                 pltpu.SemaphoreType.DMA((2,)),
                 pltpu.SemaphoreType.DMA((2,)),
-                pltpu.SemaphoreType.DMA((max(1, d_model // CHUNK),)),
                 pltpu.SemaphoreType.DMA((chunks,)),
                 pltpu.SemaphoreType.DMA((chunks,)),
             ],
             compiler_params=pltpu.CompilerParams(
-                collective_id=0, has_side_effects=True, vmem_limit_bytes=67043328),
+                collective_id=0, has_side_effects=True, vmem_limit_bytes=62849024),
         )(x_loc, w_in, a_neg[None], dt_bias[None], d_skip[None], w_out)
 
     return jax.shard_map(local_mixer, mesh=mesh, in_specs=(row_spec, P(), P(), P(), P(), P()),

time: 148 us -> 144 us (0.973)
  local copies, waits for them, and re-layouts: 4.7 us -> 2.02 us
    unnamed x1, local copies, waits for them, and re-layouts: 4.7 us -> 2.02 us
where the time goes in v3:
time: 144 us
  Pallas kernels  142 us (99%)
  local copies, waits for them, and re-layouts  2.02 us (1%)
    pallas_call x1, Pallas kernels, local_mixer(): pl.pallas_call(functools.partial(mixer_kernel, seq_devs), out_shape=pltpu...  142 us

profile of v3, /device:TPU:21, one launch (start us, length us, event | category | flops | bytes accessed | tf_op | source)
XLA Modules:
  0.0 143.8 jit_solution(4498813775640140528)
XLA Ops:
  0.0 141.8 %shard_map.64 = bf16[512,4096]{1,0:T(8,128)(2,1)S(1)} custom-call(bf16[512,4096]{1,0:T(8,128)(2,1)} %x_hbm.1, bf16[4096,16768]{1,0:T(8,128)(2,1)} %w_in.1, f32[1,128]{1,0:T(1,128)} %bitcast.3, f32[1,128]{1,0:T(1,128)} %bitcast.4, f32[1,128]{1,0:T(1,128)} %bitcast.5, bf16[8192,4096]{1,0:T(8,128)(2,1)} %w_out.1), custom_call_target="tpu_custom_call" | custom-call | tf_op jit(solution)/shard_map/pallas_call | solution.py:342
  141.8 2.0 %copy.8 = bf16[512,4096]{1,0:T(8,128)(2,1)} copy(bf16[512,4096]{1,0:T(8,128)(2,1)S(1)} %shard_map.64) | data formatting | bytes 8388608

commit v4 on v3

--- a/solution.py
+++ b/solution.py
@@ -33,7 +33,7 @@
     me = lax.axis_index("sp")
     right = lax.rem(me + 1, seq_devs)
     left = lax.rem(me + seq_devs - 1, seq_devs)
-    delay = 4 * (me // 2) + lax.rem(me, 2)
+    delay = (26 * (me // 2)) // 7 + lax.rem(me, 2)
 
     barrier = pltpu.get_barrier_semaphore()
     for peer in (left, right):
@@ -90,12 +90,10 @@
         proj = proj + jnp.dot(out_ref[:, part], win_buf[0, part, :small], preferred_element_type=f32)
     proj = proj.astype(bf16)
     win_copy(jnp.int32(2)).start()
-    first = jnp.zeros((tokens, CHUNK), f32)
     for piece in range(PIECES):
         first_copy(piece).wait()
-        part = slice(k_tile * piece, k_tile * (piece + 1))
-        first = first + jnp.dot(out_ref[:, part], win_buf[1, part, :], preferred_element_type=f32)
-    xs_buf[:, :CHUNK] = first.astype(bf16)
+    head, tail = slice(0, d_model // 2), slice(d_model // 2, d_model)
+    first = jnp.dot(out_ref[:, head], win_buf[1, head, :], preferred_element_type=f32)
     c_buf[...] = proj[:, state:2 * state]
     bt_buf[...] = proj[:, :state].astype(f32).T.astype(bf16)
     dt = jax.nn.softplus(proj[:, 2 * state:].astype(f32) + dt_bias[...])
@@ -118,6 +116,8 @@
     row_buf[segs:segs + 1, :] = jnp.exp(total)
     row_buf[segs + 1:segs + 2, :] = d_skip[...]
     row_buf[segs + 2:8, :] = jnp.zeros((8 - segs - 2, heads), f32)
+    first = first + jnp.dot(out_ref[:, tail], win_buf[1, tail, :], preferred_element_type=f32)
+    xs_buf[:, :CHUNK] = first.astype(bf16)
 
     def low_half(rows):
         return lax.broadcasted_iota(jnp.int32, (rows, LANES), 1) < head_dim
@@ -162,10 +162,15 @@
                            + seg_state(xw_buf[SEG_LEN * seg:SEG_LEN * (seg + 1), :], seg))
         s_buf[chunk] = total_state
 
+    def relayed(step):
+        turn = step - 3 - delay
+        chunk = turn - turn // 7
+        return chunk, (turn >= 0) & (lax.rem(turn, 7) != 6) & (chunk < chunks)
+
     def relay(step):
-        chunk = step - 3 - delay
-
-        @pl.when((chunk >= 0) & (chunk < chunks))
+        chunk, active = relayed(step)
+
+        @pl.when(active)
         def _():
             @pl.when(me > 0)
             def _():
@@ -177,9 +182,9 @@
                 s_buf[chunk] = decay * h_buf[chunk] + s_buf[chunk]
 
     def forward(step):
-        chunk = step - 3 - delay
-
-        @pl.when((chunk >= 0) & (chunk < chunks) & (me < seq_devs - 1))
+        chunk, active = relayed(step)
+
+        @pl.when(active & (me < seq_devs - 1))
         def _():
             state_copy(chunk).start()
 
@@ -188,7 +193,7 @@
         target[:, columns_of(chunk)] = jnp.dot(
             out_ref[...], win_buf[slot], preferred_element_type=f32).astype(bf16)
 
-    def ssd_seg(chunk, seg, state_now, gated):
+    def ssd_seg(chunk, seg, state_now, gated, middle):
         columns = columns_of(chunk)
         table = decay_buf.at[chunk]
         low = low_half(SEG_LEN)
@@ -204,6 +209,8 @@
         scores = cb_buf[rows, :]
         causal = row_i >= col_i
         for pair in range(heads_chunk // 2):
+            if pair == heads_chunk // 4:
+                middle()
             lanes = slice(LANES * pair, LANES * (pair + 1))
             logs_pair, mats = [], []
             for head in (2 * pair, 2 * pair + 1):
@@ -226,8 +233,8 @@
     def mix_and_add(chunk, gated, piece_of):
         state_now = h_buf[chunk]
         for seg in range(segs):
-            piece_of(seg)
-            state_now = ssd_seg(chunk, seg, state_now, gated)
+            piece_of(2 * seg)
+            state_now = ssd_seg(chunk, seg, state_now, gated, lambda: piece_of(2 * seg + 1))
 
     pl.semaphore_wait(barrier, 2)
 
@@ -276,16 +283,16 @@
     acc[:, cleared * (chunks - 1):] = jnp.zeros((tokens, cleared), f32)
 
     def z_piece(seg):
-        if seg % 2 == 0:
+        if seg % segs == 0:
             width = 2 * CHUNK // segs
-            start = width * (seg // 2)
+            start = width * (seg // segs)
             z_buf[:, inner - CHUNK + start:inner - CHUNK + start + width] = jnp.dot(
                 out_ref[...], win_buf[(2 * chunks) % 2, :, start:start + width], preferred_element_type=f32).astype(bf16)
 
     mix_and_add(0, gated_a, z_piece)
 
     def out_part(chunk, gated, piece):
-        width = d_model // segs
+        width = d_model // (2 * segs)
         cols = slice(width * piece, width * (piece + 1))
         slot = chunk % 2 if isinstance(chunk, int) else lax.rem(chunk, 2)
         acc[:, cols] += jnp.dot(gated[...], wout_buf[slot, :, cols], preferred_element_type=f32)

time: 144 us -> 143 us (level)
  no operation moved by 1% of the time
where the time goes in v4:
time: 143 us
  Pallas kernels  141 us (99%)
  local copies, waits for them, and re-layouts  2.02 us (1%)
    pallas_call x1, Pallas kernels, local_mixer(): pl.pallas_call(functools.partial(mixer_kernel, seq_devs), out_shape=pltpu...  141 us

profile of v4, /device:TPU:21, one launch (start us, length us, event | category | flops | bytes accessed | tf_op | source)
XLA Modules:
  0.0 143.1 jit_solution(1624152720688217229)
XLA Ops:
  0.0 141.1 %shard_map.64 = bf16[512,4096]{1,0:T(8,128)(2,1)S(1)} custom-call(bf16[512,4096]{1,0:T(8,128)(2,1)} %x_hbm.1, bf16[4096,16768]{1,0:T(8,128)(2,1)} %w_in.1, f32[1,128]{1,0:T(1,128)} %bitcast.3, f32[1,128]{1,0:T(1,128)} %bitcast.4, f32[1,128]{1,0:T(1,128)} %bitcast.5, bf16[8192,4096]{1,0:T(8,128)(2,1)} %w_out.1), custom_call_target="tpu_custom_call" | custom-call | tf_op jit(solution)/shard_map/pallas_call | solution.py:349
  141.1 2.0 %copy.8 = bf16[512,4096]{1,0:T(8,128)(2,1)} copy(bf16[512,4096]{1,0:T(8,128)(2,1)S(1)} %shard_map.64) | data formatting | bytes 8388608

commit v5 on v4

--- a/solution.py
+++ b/solution.py
@@ -33,7 +33,9 @@
     me = lax.axis_index("sp")
     right = lax.rem(me + 1, seq_devs)
     left = lax.rem(me + seq_devs - 1, seq_devs)
-    delay = (26 * (me // 2)) // 7 + lax.rem(me, 2)
+    chip = me // 2
+    later = (chip + 7) // 8
+    delay = (7 * chip + 3 * later) // 2 + lax.rem(me, 2) * (3 - 2 * later)
 
     barrier = pltpu.get_barrier_semaphore()
     for peer in (left, right):

time: 143 us -> 142 us (level); the launches traced: 143 us -> 140 us
  Pallas kernels: 141 us -> 138 us
    pallas_call x1, Pallas kernels: 141 us -> 138 us  [local_mixer(): pl.pallas_call(functools.partial(mixer_kernel, seq_devs), out_shape=pltpu...]
where the time goes in v5:
time: 142 us; the launch traced here: 140 us
  Pallas kernels  138 us (97%)
  local copies, waits for them, and re-layouts  2.02 us (1%)
    pallas_call x1, Pallas kernels, local_mixer(): pl.pallas_call(functools.partial(mixer_kernel, seq_devs), out_shape=pltpu...  138 us

profile of v5, /device:TPU:21, one launch (start us, length us, event | category | flops | bytes accessed | tf_op | source)
XLA Modules:
  0.0 139.8 jit_solution(11432617111897052126)
XLA Ops:
  0.0 137.8 %shard_map.64 = bf16[512,4096]{1,0:T(8,128)(2,1)S(1)} custom-call(bf16[512,4096]{1,0:T(8,128)(2,1)} %x_hbm.1, bf16[4096,16768]{1,0:T(8,128)(2,1)} %w_in.1, f32[1,128]{1,0:T(1,128)} %bitcast.3, f32[1,128]{1,0:T(1,128)} %bitcast.4, f32[1,128]{1,0:T(1,128)} %bitcast.5, bf16[8192,4096]{1,0:T(8,128)(2,1)} %w_out.1), custom_call_target="tpu_custom_call" | custom-call | tf_op jit(solution)/shard_map/pallas_call | solution.py:351
  137.8 2.0 %copy.8 = bf16[512,4096]{1,0:T(8,128)(2,1)} copy(bf16[512,4096]{1,0:T(8,128)(2,1)S(1)} %shard_map.64) | data formatting | bytes 8388608
